TPU v7x, 32 devices: a whole 2x2x4 slice. The times are simulated.
32 devices in a mesh: seq: 8 (over y, x, core), vocab: 4 (over z).
Axes of the slice: x: 2, y: 2, z: 4, core: 2. Of those that a mesh axis runs over, the one named last changes fastest.
Arguments:
- hidden: bfloat16 [960, 4096], P('seq'), may hold values from -32 to 32
- head_weight: bfloat16 [4096, 98304], P(None, ('seq', 'vocab')), may hold values from -0.84375 to 0.84375
- labels: int32 [960], P('seq'), may hold values from 0 to 98303
- lengths: int32 [8], replicated, may hold values from 1 to 120, 480 in all
- pair_map: int32 [8], replicated, may hold values from 0 to 7, each once
- ref_margin: float32 [4], replicated, may hold values from -240 to 240
Outputs:
- seq_logps: float32 [8], replicated
- pair_loss: float32 [4], replicated
- z_loss: float32 [], replicated
Inputs may be any that keep to these rules, and one draw needn't show every extreme that they name: The lengths sum to 480 and the longest is exactly 120. Each response appears once; pair p compares response pair_map[2p], chosen, with response pair_map[2p+1], rejected.
All inputs are finite; a program needn't handle non-finite values.
Results may differ from a plain program's by a relative error of at most 0.0003.
Values may be sent and summed in bfloat16 or wider, within the bound.
No kernel may reach another device: no remote copies, remote signals or barrier semaphores. Data moves between devices by JAX's collectives and lax.ppermute only.
A program may use at most 192 MiB of HBM per device.

v0:
```python
import jax
import jax.numpy as jnp
from jax import lax
from jax.sharding import PartitionSpec as P

pref_beta = 0.05
zloss_weight = 0.0001


def per_device(hidden, head_weight, labels, lengths, pair_map, ref_margin):
    vocab_devices = lax.axis_size("vocab")
    shard_rows = hidden.shape[0]
    columns = head_weight.shape[1]
    seq_total = lengths.shape[0]
    col_first = (lax.axis_index("seq") * vocab_devices + lax.axis_index("vocab")) * columns
    col_ids = col_first + jnp.arange(columns, dtype=jnp.int32)
    seq_ids = jnp.arange(seq_total, dtype=jnp.int32)
    logits = jnp.dot(
        lax.all_gather(hidden, "seq", axis=0, tiled=True),
        head_weight,
        preferred_element_type=jnp.float32,
    )
    local_max = jnp.max(logits, axis=1)
    local_sum = jnp.sum(jnp.exp(logits - local_max[:, None]), axis=1)
    picked = jnp.sum(
        jnp.where(
            lax.all_gather(labels, "seq", axis=0, tiled=True)[:, None] == col_ids[None, :],
            logits,
            0.0,
        ),
        axis=1,
    )
    fresh = (local_max, local_sum, picked)
    local_max, local_sum, picked = tuple((fresh_part for fresh_part in fresh))
    top_score = lax.pmax(local_max, ("seq", "vocab"))
    exp_total, label_logit = lax.psum(
        (local_sum * jnp.exp(local_max - top_score), picked), ("seq", "vocab")
    )
    log_norm = (top_score + jnp.log(exp_total)).reshape(seq_total, shard_rows)
    label_logit = label_logit.reshape(seq_total, shard_rows)
    live_mask = jnp.arange(shard_rows, dtype=jnp.int32)[None, :] < lengths[:, None]
    seq_logps = jnp.sum(jnp.where(live_mask, label_logit - log_norm, 0.0), axis=1)
    select = (pair_map[:, None] == seq_ids[None, :]).astype(jnp.float32)
    ordered = jnp.dot(select, seq_logps, precision=lax.Precision.HIGHEST).reshape(seq_total // 2, 2)
    pair_loss = jax.nn.softplus(-pref_beta * (ordered[:, 0] - ordered[:, 1] - ref_margin))
    live_count = jnp.sum(live_mask.astype(jnp.float32))
    z_loss = zloss_weight * jnp.sum(jnp.where(live_mask, log_norm * log_norm, 0.0)) / live_count
    return (seq_logps, pair_loss, z_loss)


def solution(mesh):
    placed = (P("seq", None), P(None, ("seq", "vocab")), P("seq"), P(), P(), P())
    return jax.shard_map(
        per_device, mesh=mesh, in_specs=placed, out_specs=(P(), P(), P()), check_vma=False
    )
```

profile of v0, /device:TPU:0, one launch (start us, length us, event | category | flops | bytes accessed | tf_op | source)
XLA Modules:
  0.0 195.6 jit_solution(578517166683249568)
XLA Ops:
  7.2 0.0 all-gather.2.cloned.1.call-start
  7.2 0.7 all-gather.2.cloned.1.call-update
  7.9 0.7 iota_compare_fusion
  8.6 0.1 lt.20
  8.7 0.7 eq.32
  9.5 1.2 dynamic-slice
  11.4 0.9 dynamic-update-slice
  12.2 9.5 %all-reduce = s32[960]{0:T(1024)S(1)} all-reduce(s32[960]{0:T(1024)S(1)} %dynamic-update-slice), channel_id=1, replica_groups=mesh['seq'=8,'vocab'=4] {'seq'}, use_global_device_ids=true, to_apply=%add | all-reduce | flops 960 | bytes 7680
  21.7 42.9 %all-gather.2.cloned.1.call-done = bf16[960,4096]{1,0:T(8,128)(2,1)} async-done(((bf16[120,4096]{1,0:T(8,128)(2,1)}), bf16[960,4096]{1,0:T(8,128)(2,1)}) %all-gather.2.cloned.1.call-update) | async-done | bytes 7864336 | tf_op jit(solution)/shard_map/all_gather | solution.py:19
  64.7 32.4 %fusion.7 = (f32[960]{0:T(1024)S(1)}, f32[960,3072]{1,0:T(8,128)}) fusion(bf16[960,4096]{1,0:T(8,128)(2,1)} %all-gather.2.cloned.1.call-done, bf16[4096,3072]{1,0:T(8,128)(2,1)} %param.7), kind=kOutput, calls=%fused_computation.18 | convolution fusion | flops 24162140160 | bytes 44830464 | tf_op jit(solution)/shard_map/dot_general | solution.py:18
  97.1 0.0 copy-start.1
  97.1 0.0 copy-start
  97.1 39.3 %pmax.7 = f32[960]{0:T(1024)S(1)} all-reduce(f32[960]{0:T(1024)S(1)} %get-tuple-element.11), channel_id=1, replica_groups=mesh['seq'=8,'vocab'=4] {'seq','vocab'}, use_global_device_ids=true, to_apply=%region_3.4 | all-reduce | flops 960 | bytes 7680 | tf_op jit(solution)/shard_map/pmax | solution.py:35
  136.4 6.4 %exponential_reduce_fusion = (f32[960]{0:T(1024)S(1)}, f32[960]{0:T(1024)S(1)}) fusion(f32[960,3072]{1,0:T(8,128)} %get-tuple-element.12, f32[960]{0:T(1024)S(1)} %get-tuple-element.11, s32[3072]{0:T(1024)S(1)} %iota_add_fusion, s32[960]{0:T(1024)S(1)} %all-reduce), kind=kLoop, calls=%fused_computation | loop fusion | flops 14743680 | bytes 11824128 | tf_op jit(solution)/shard_map/reduce_sum | solution.py:24
  142.8 41.1 %all-reduce.1 = (f32[960]{0:T(1024)S(1)}, f32[960]{0:T(1024)S(1)}) all-reduce(f32[960]{0:T(1024)S(1)} %get-tuple-element.4, f32[960]{0:T(1024)S(1)} %exponential_multiply_fusion), channel_id=1, replica_groups=mesh['seq'=8,'vocab'=4] {'seq','vocab'}, use_global_device_ids=true, to_apply=%region_1.0 | all-reduce | flops 1920 | bytes 15360 | tf_op jit(solution)/shard_map/psum | solution.py:36
  183.8 0.6 select_reduce_fusion.1
  184.5 0.1 sub.30
  184.5 0.0 copy-done.1
  184.5 0.7 convert_reduce_fusion
  185.3 0.0 copy-start.2
  185.3 0.3 fusion
  185.6 0.1 copy.9
  185.7 0.0 copy-done
  185.7 0.5 compare_select_fusion
  187.6 0.0 copy-done.2
  (3 shorter events, 0.0 us)
Async XLA Ops:
  7.2 57.5 %all-gather.2.cloned.1.call-start = ((), (), s32[]{:S(2)}) async-start(), calls=%async_computation | async-start | bytes 8847360 | tf_op jit(solution)/shard_map/all_gather | solution.py:19
  97.1 87.4 %copy-start.1 = (s32[8]{0:T(128)S(1)}, s32[8]{0:T(128)}, u32[]{:S(2)}) copy-start(s32[8]{0:T(128)} %param.9) | copy-start | bytes 100
  97.1 88.6 %copy-start = (f32[4]{0:T(128)S(1)}, f32[4]{0:T(128)}, u32[]{:S(2)}) copy-start(f32[4]{0:T(128)} %param.11) | copy-start | bytes 52
  185.3 2.3 %copy-start.2 = (f32[8]{0:T(128)}, f32[8]{0:T(128)S(1)}, u32[]{:S(2)}) copy-start(f32[8]{0:T(128)S(1)} %get-tuple-element.6) | copy-start | bytes 100
Sparse Core Ops, SparseCore 0:
  9.9 54.7 all-gather.1
where the time goes:
time: 196 us
  blocking collectives  89.8 us (46%)
  waiting for transfers between devices  43.6 us (22%)
  matrix products  32.7 us (17%)
  between operations  17.2 us (9%)
  other arithmetic  9.04 us (5%)
  local copies, waits for them, and re-layouts  3.11 us (2%)
    all_gather x1, waiting for transfers between devices, per_device(): lax.all_gather(hidden, 'seq', axis=0, tiled=True)  42.9 us
    psum x1, blocking collectives, per_device(): lax.psum((local_sum * jnp.exp(local_max - top_score), picked), ('seq', 'v...  41.1 us
    pmax x1, blocking collectives, per_device(): top_score = lax.pmax(local_max, ('seq', 'vocab'))  39.3 us
    dot_general x1, matrix products, per_device(): jnp.dot(lax.all_gather(hidden, 'seq', axis=0, tiled=True), head_weight, p...  32.4 us
    unnamed x1, blocking collectives  9.49 us
    reduce_sum x1, other arithmetic, per_device(): local_sum = jnp.sum(jnp.exp(logits - local_max[:, None]), axis=1)  6.39 us
  transfers between devices with their start and end apart: 1, of which 1 were waited for; matrix products, arithmetic and copies ran while one was open for 2% of the time, Pallas kernels for 0%

commit v1 on v0

--- a/solution.py
+++ b/solution.py
@@ -5,6 +5,14 @@
 
 pref_beta = 0.05
 zloss_weight = 0.0001
+
+
+def begin_the_vector(state):
+    which_axis = "vocab"
+    peer_axis = "seq"
+    for hop_no in (which_axis, peer_axis):
+        state = lax.psum(state, hop_no)
+    return state
 
 
 def per_device(hidden, head_weight, labels, lengths, pair_map, ref_margin):
@@ -33,9 +41,7 @@
     fresh = (local_max, local_sum, picked)
     local_max, local_sum, picked = tuple((fresh_part for fresh_part in fresh))
     top_score = lax.pmax(local_max, ("seq", "vocab"))
-    exp_total, label_logit = lax.psum(
-        (local_sum * jnp.exp(local_max - top_score), picked), ("seq", "vocab")
-    )
+    exp_total, label_logit = begin_the_vector((local_sum * jnp.exp(local_max - top_score), picked))
     log_norm = (top_score + jnp.log(exp_total)).reshape(seq_total, shard_rows)
     label_logit = label_logit.reshape(seq_total, shard_rows)
     live_mask = jnp.arange(shard_rows, dtype=jnp.int32)[None, :] < lengths[:, None]

time: 196 us -> 178 us (0.908)
  blocking collectives: 89.8 us -> 71.7 us
    psum x1 -> x2, blocking collectives: 41.1 us -> 23 us  [begin_the_vector(): state = lax.psum(state, hop_no)]
where the time goes in v1:
time: 178 us; the launch traced here: 177 us
  blocking collectives  71.7 us (40%)
  waiting for transfers between devices  43.6 us (24%)
  matrix products  32.7 us (18%)
  between operations  17.3 us (10%)
  other arithmetic  9.04 us (5%)
  local copies, waits for them, and re-layouts  3.11 us (2%)
    all_gather x1, waiting for transfers between devices, per_device(): lax.all_gather(hidden, 'seq', axis=0, tiled=True)  42.9 us
    pmax x1, blocking collectives, per_device(): top_score = lax.pmax(local_max, ('seq', 'vocab'))  39.2 us
    dot_general x1, matrix products, per_device(): jnp.dot(lax.all_gather(hidden, 'seq', axis=0, tiled=True), head_weight, p...  32.4 us
    psum x2, blocking collectives, begin_the_vector(): state = lax.psum(state, hop_no)  23 us
    unnamed x1, blocking collectives  9.49 us
    reduce_sum x1, other arithmetic, per_device(): local_sum = jnp.sum(jnp.exp(logits - local_max[:, None]), axis=1)  6.39 us
  transfers between devices with their start and end apart: 1, of which 1 were waited for; matrix products, arithmetic and copies ran while one was open for 2% of the time, Pallas kernels for 0%

profile of v1, /device:TPU:0, one launch (start us, length us, event | category | flops | bytes accessed | tf_op | source)
XLA Modules:
  0.0 177.5 jit_solution(12035920809394591059)
XLA Ops:
  7.2 0.0 all-gather.2.cloned.1.call-start
  7.2 0.7 all-gather.2.cloned.1.call-update
  7.9 0.7 iota_compare_fusion
  8.6 0.1 lt.20
  8.7 0.7 eq.32
  9.5 1.2 dynamic-slice
  11.4 0.9 dynamic-update-slice
  12.2 9.5 %all-reduce = s32[960]{0:T(1024)S(1)} all-reduce(s32[960]{0:T(1024)S(1)} %dynamic-update-slice), channel_id=1, replica_groups=mesh['seq'=8,'vocab'=4] {'seq'}, use_global_device_ids=true, to_apply=%add | all-reduce | flops 960 | bytes 7680
  21.7 42.9 %all-gather.2.cloned.1.call-done = bf16[960,4096]{1,0:T(8,128)(2,1)} async-done(((bf16[120,4096]{1,0:T(8,128)(2,1)}), bf16[960,4096]{1,0:T(8,128)(2,1)}) %all-gather.2.cloned.1.call-update) | async-done | bytes 7864336 | tf_op jit(solution)/shard_map/all_gather | solution.py:27
  64.7 32.4 %fusion.7 = (f32[960]{0:T(1024)S(1)}, f32[960,3072]{1,0:T(8,128)}) fusion(bf16[960,4096]{1,0:T(8,128)(2,1)} %all-gather.2.cloned.1.call-done, bf16[4096,3072]{1,0:T(8,128)(2,1)} %param.7), kind=kOutput, calls=%fused_computation.18 | convolution fusion | flops 24162140160 | bytes 44830464 | tf_op jit(solution)/shard_map/dot_general | solution.py:26
  97.1 0.0 copy-start.1
  97.1 0.0 copy-start
  97.1 39.2 %pmax.7 = f32[960]{0:T(1024)S(1)} all-reduce(f32[960]{0:T(1024)S(1)} %get-tuple-element.13), channel_id=1, replica_groups=mesh['seq'=8,'vocab'=4] {'seq','vocab'}, use_global_device_ids=true, to_apply=%region_4.5 | all-reduce | flops 960 | bytes 7680 | tf_op jit(solution)/shard_map/pmax | solution.py:43
  136.3 6.4 %exponential_reduce_fusion = (f32[960]{0:T(1024)S(1)}, f32[960]{0:T(1024)S(1)}) fusion(f32[960,3072]{1,0:T(8,128)} %get-tuple-element.14, f32[960]{0:T(1024)S(1)} %get-tuple-element.13, s32[3072]{0:T(1024)S(1)} %iota_add_fusion, s32[960]{0:T(1024)S(1)} %all-reduce), kind=kLoop, calls=%fused_computation | loop fusion | flops 14743680 | bytes 11824128 | tf_op jit(solution)/shard_map/reduce_sum | solution.py:32
  142.8 10.8 %all-reduce.2 = (f32[960]{0:T(1024)S(1)}, f32[960]{0:T(1024)S(1)}) all-reduce(f32[960]{0:T(1024)S(1)} %get-tuple-element.4, f32[960]{0:T(1024)S(1)} %exponential_multiply_fusion), channel_id=1, replica_groups=mesh['seq'=8,'vocab'=4] {'vocab'}, use_global_device_ids=true, to_apply=%region_1.0 | all-reduce | flops 1920 | bytes 15360 | tf_op jit(solution)/shard_map/psum | solution.py:14
  153.5 12.2 %all-reduce.1 = (f32[960]{0:T(1024)S(1)}, f32[960]{0:T(1024)S(1)}) all-reduce(f32[960]{0:T(1024)S(1)} %get-tuple-element.9, f32[960]{0:T(1024)S(1)} %get-tuple-element.10), channel_id=1, replica_groups=mesh['seq'=8,'vocab'=4] {'seq'}, use_global_device_ids=true, to_apply=%region_2.3 | all-reduce | flops 1920 | bytes 15360 | tf_op jit(solution)/shard_map/psum | solution.py:14
  165.7 0.6 select_reduce_fusion.1
  166.3 0.1 sub.30
  166.4 0.0 copy-done.1
  166.4 0.7 convert_reduce_fusion
  167.2 0.0 copy-start.2
  167.2 0.3 fusion
  167.5 0.1 copy.9
  167.6 0.0 copy-done
  167.6 0.5 compare_select_fusion
  169.5 0.0 copy-done.2
  (3 shorter events, 0.0 us)
Async XLA Ops:
  7.2 57.5 %all-gather.2.cloned.1.call-start = ((), (), s32[]{:S(2)}) async-start(), calls=%async_computation | async-start | bytes 8847360 | tf_op jit(solution)/shard_map/all_gather | solution.py:27
  97.1 69.3 %copy-start.1 = (s32[8]{0:T(128)S(1)}, s32[8]{0:T(128)}, u32[]{:S(2)}) copy-start(s32[8]{0:T(128)} %param.9) | copy-start | bytes 100
  97.1 70.5 %copy-start = (f32[4]{0:T(128)S(1)}, f32[4]{0:T(128)}, u32[]{:S(2)}) copy-start(f32[4]{0:T(128)} %param.11) | copy-start | bytes 52
  167.2 2.3 %copy-start.2 = (f32[8]{0:T(128)}, f32[8]{0:T(128)S(1)}, u32[]{:S(2)}) copy-start(f32[8]{0:T(128)S(1)} %get-tuple-element.6) | copy-start | bytes 100
Sparse Core Ops, SparseCore 0:
  9.9 54.7 all-gather.1
